TPU v7x, 32 devices: a whole 2x2x4 slice. The times are simulated.
32 devices in a mesh: grp: 2 (over y), seq: 4 (over z), head: 4 (over x, core).
Axes of the slice: x: 2, y: 2, z: 4, core: 2. Of those that a mesh axis runs over, the one named last changes fastest.
Arguments:
- queries: bfloat16 [1024, 32, 128], P(('grp', 'seq'), 'head'), parts along dimension 0, may hold values from -26 to 26
- keys: bfloat16 [1024, 8, 128], P(('grp', 'seq'), 'head'), parts along dimension 0, may hold values from -13 to 13
- values: bfloat16 [1024, 8, 128], P(('grp', 'seq'), 'head'), parts along dimension 0, may hold values from -6 to 6
- block_order: int32 [16], P('grp'), parts along dimension 0, may hold values from 0 to 7, as said below
Outputs:
- attended: bfloat16 [1024, 32, 128], P(('grp', 'seq'), 'head'), parts along dimension 0
There are 2 independent parts, one for each index of `grp`. A program takes and returns all parts, laid end to end along the dimension named above; each array names one. Nothing has to cross between parts.
Inputs may be any that keep to these rules, and one draw needn't show every extreme that they name: `block_order`: slots 2 i and 2 i + 1 hold blocks c and 7 - c for some c, in either order; every block stands in one slot.
All inputs are finite; a program needn't handle non-finite values.
Results may differ from a plain program's by a relative error of at most 0.0055.
Values may be sent and summed in bfloat16 or wider, within the bound.
A program may use at most 128 MiB of HBM per device.

v0:
```python
import functools
import math

import jax
import jax.numpy as jnp
from jax import lax
from jax.experimental import pallas as pl
from jax.experimental.pallas import tpu as pltpu
from jax.sharding import PartitionSpec as P

MESH = pl.DeviceIdType.MESH
NEG = -1e30


def gather_attend(
    n,
    heads,
    groups,
    tile,
    table_hbm,
    q_hbm,
    k_hbm,
    v_hbm,
    out_ref,
    table_ref,
    q_ref,
    kv_ref,
    p_ref,
    m_ref,
    l_ref,
    acc_ref,
    load_sem,
    send_sem,
    recv_sem,
):
    me = lax.axis_index("seq")
    rows, width = q_ref.shape
    tokens = rows // heads
    half = tokens // 2
    per_group = heads // groups
    cols = tokens * groups
    piece = cols // 2
    factor_scale = width ** (-0.5) * math.log2(math.e)
    right, left = me + 1, me - 1
    has_right, has_left = me < n - 1, me > 0
    early = True
    barrier = pltpu.get_barrier_semaphore()

    @pl.when(has_right)
    def _():
        pl.semaphore_signal(barrier, inc=1, device_id={"seq": right}, device_id_type=MESH)

    @pl.when(has_left)
    def _():
        pl.semaphore_signal(barrier, inc=1, device_id={"seq": left}, device_id_type=MESH)

    loads = [
        pltpu.make_async_copy(k_hbm, kv_ref.at[me, 0], load_sem.at[0]),
        pltpu.make_async_copy(v_hbm, kv_ref.at[me, 1], load_sem.at[1]),
        pltpu.make_async_copy(table_hbm, table_ref, load_sem.at[2]),
        pltpu.make_async_copy(q_hbm, q_ref, load_sem.at[3]),
    ]
    for load in loads:
        load.start()

    pl.semaphore_wait(barrier, has_right.astype(jnp.int32) + has_left.astype(jnp.int32))

    def remote(shard, which, way):
        part = kv_ref.at[shard, which // 2, pl.ds((which % 2) * piece, piece)]
        return pltpu.make_async_remote_copy(
            src_ref=part,
            dst_ref=part,
            send_sem=send_sem.at[way, shard, which],
            recv_sem=recv_sem.at[shard, which],
            device_id={"seq": left if way else right},
            device_id_type=MESH,
        )

    for which in range(4):
        if which % 2 == 0:
            loads[which // 2].wait()

        @pl.when(has_right)
        def _():
            remote(me, which, 0).start()

        @pl.when(has_left)
        def _():
            remote(me, which, 1).start()

    m_ref[...] = jnp.full(m_ref.shape, NEG, jnp.float32)
    l_ref[...] = jnp.zeros(l_ref.shape, jnp.float32)
    acc_ref[...] = jnp.zeros(acc_ref.shape, jnp.float32)
    loads[2].wait()
    loads[3].wait()

    lane = lax.broadcasted_iota(jnp.int32, (heads, cols), 1)
    head = lax.broadcasted_iota(jnp.int32, (heads, cols), 0)
    matched = lane % groups == head // per_group
    key_token = lane // groups

    def take(distance, which):
        from_left, from_right = me - distance, me + distance

        @pl.when(from_left >= 0)
        def _():
            remote(from_left, which, 0).wait_recv()

            @pl.when(has_right)
            def _():
                remote(from_left, which, 0).start()

        @pl.when(from_right < n)
        def _():
            remote(from_right, which, 1).wait_recv()

            @pl.when(has_left)
            def _():
                remote(from_right, which, 1).start()

    def scores(shard, section, start):
        span = pl.ds(pl.multiple_of((section * half + start) * heads, tile * heads), tile * heads)
        first, second = table_ref[2 * shard], table_ref[2 * shard + 1]
        key_pos = jnp.where(
            key_token < half, first * half + key_token, (second - 1) * half + key_token
        )
        key_code = jnp.where(matched, key_pos, 2**30)
        offset = table_ref[2 * me + section] * half + start
        raw = lax.dot_general(
            q_ref[span, :],
            kv_ref[shard, 0],
            (((1,), (1,)), ((), ())),
            preferred_element_type=jnp.float32,
        )
        shaped = raw.reshape(tile, heads, cols)
        query_pos = lax.broadcasted_iota(jnp.int32, shaped.shape, 0) + offset
        shaped = jnp.where(key_code[None] <= query_pos, shaped, NEG)
        raw = shaped.reshape(tile * heads, cols)
        old_max = m_ref[span, :]
        new_max = jnp.maximum(old_max, jnp.max(raw, axis=-1, keepdims=True))
        fade = jnp.exp2((old_max - new_max) * factor_scale)
        total = l_ref[span, :] * fade
        pieces = []
        for low in range(0, cols, width):
            weights = jnp.exp2((raw[:, low : low + width] - new_max) * factor_scale)
            total += weights
            pieces.append(weights.astype(p_ref.dtype))
        m_ref[span, :] = new_max
        l_ref[span, :] = total
        return span, jnp.concatenate(pieces, axis=1), fade

    def both(shard, section, start):
        span, weights, fade = scores(shard, section, start)
        acc_ref[span, :] = acc_ref[span, :] * fade + jnp.dot(
            weights, kv_ref[shard, 1], preferred_element_type=jnp.float32
        )

    def whole(shard):
        def section_of(section, carry):
            for start in range(0, half, tile):
                both(shard, section, start)
            return carry

        lax.fori_loop(0, 2, section_of, 0)

    whole(me)

    def at(index, way):
        return jnp.where(way == 0, me - index, me + index)

    def relay_round(distance, carry):
        def side(way):
            shard = at(distance - 1, way)

            @pl.when((distance > 1) & (shard >= 0) & (shard < n))
            def _():
                whole(shard)

        if early:
            side(0)
        for which in range(4):
            take(distance, which)
        if not early:
            side(0)
        side(1)
        return carry

    def end_round(distance, carry):
        shard = jnp.where(has_left, me - distance, me + distance)
        for which in range(4):
            take(distance, which)
        whole(shard)
        return carry

    def settle(distance, carry):
        for which in range(4):

            @pl.when((me - distance >= 0) & has_right)
            def _():
                remote(me - distance, which, 0).wait_send()

            @pl.when((me + distance < n) & has_left)
            def _():
                remote(me + distance, which, 1).wait_send()

        return carry

    def close():
        for start in range(0, tokens, tile):
            span = pl.ds(start * heads, tile * heads)
            scale = 1.0 / jnp.sum(l_ref[span, :], axis=-1, keepdims=True)
            out_ref[span, :] = (acc_ref[span, :] * scale).astype(out_ref.dtype)

    if n == 1:
        close()
        return

    interior = has_left & has_right

    @pl.when(interior)
    def _():
        lax.fori_loop(1, n - 1, relay_round, 0)
        lax.fori_loop(0, n - 2, settle, 0)
        relay_round(n - 1, 0)
        close()
        settle(n - 2, 0)

    @pl.when(jnp.logical_not(interior))
    def _():
        lax.fori_loop(1, n - 1, end_round, 0)
        settle(0, 0)
        last = n - 1 - me
        for which in (0, 1):
            take(n - 1, which)
        for start in range(0, tokens, tile):
            span, weights, fade = scores(last, start // half, start % half)
            scale = 1.0 / jnp.sum(l_ref[span, :], axis=-1, keepdims=True)
            p_ref[span, :] = weights
            acc_ref[span, :] = acc_ref[span, :] * (fade * scale)
            l_ref[span, :] = jnp.broadcast_to(scale, (tile * heads, width))
        for which in (2, 3):
            take(n - 1, which)
        for start in range(0, tokens, tile):
            span = pl.ds(start * heads, tile * heads)
            product = jnp.dot(p_ref[span, :], kv_ref[last, 1], preferred_element_type=jnp.float32)
            out_ref[span, :] = (acc_ref[span, :] + product * l_ref[span, :]).astype(out_ref.dtype)


def on_device(queries, keys, values, block_order):
    n = lax.axis_size("seq")
    tokens, heads, width = queries.shape
    groups = keys.shape[1]
    rows, cols = tokens * heads, tokens * groups
    tile = min(64, tokens // 2)
    anywhere = pl.BlockSpec(memory_space=pltpu.HBM)
    out = pl.pallas_call(
        functools.partial(gather_attend, n, heads, groups, tile),
        out_shape=pltpu.VMEM((rows, width), queries.dtype),
        in_specs=[anywhere] * 4,
        out_specs=pl.BlockSpec(memory_space=pltpu.VMEM),
        scratch_shapes=[
            pltpu.SMEM(block_order.shape, block_order.dtype),
            pltpu.VMEM((rows, width), queries.dtype),
            pltpu.VMEM((n, 2, cols, width), keys.dtype),
            pltpu.VMEM((rows, cols), values.dtype),
            pltpu.VMEM((rows, width), jnp.float32),
            pltpu.VMEM((rows, width), jnp.float32),
            pltpu.VMEM((rows, width), jnp.float32),
            pltpu.SemaphoreType.DMA((4,)),
            pltpu.SemaphoreType.DMA((2, n, 4)),
            pltpu.SemaphoreType.DMA((n, 4)),
        ],
        compiler_params=pltpu.CompilerParams(collective_id=0, has_side_effects=True),
    )(
        block_order,
        queries.reshape(rows, width),
        keys.reshape(cols, width),
        values.reshape(cols, width),
    )
    return out.reshape(tokens, heads, width)


def solution(mesh):
    placed = P(("grp", "seq"), "head", None)
    return jax.shard_map(
        on_device,
        mesh=mesh,
        in_specs=(placed, placed, placed, P("grp")),
        out_specs=placed,
        check_vma=False,
    )
```

profile of v0, /device:TPU:0, one launch (start us, length us, event | category | flops | bytes accessed | tf_op | source)
XLA Modules:
  0.0 15.8 jit_solution(10205326000518844056)
XLA Ops:
  0.0 15.1 %shard_map.46 = bf16[1024,128]{1,0:T(8,128)(2,1)S(1)} custom-call(s32[8]{0:T(128)} %table_hbm.1, bf16[1024,128]{1,0:T(8,128)(2,1)} %bitcast.5, bf16[256,128]{1,0:T(8,128)(2,1)} %bitcast.6, bf16[256,128]{1,0:T(8,128)(2,1)} %bitcast.7), custom_call_target="tpu_custom_call" | custom-call | tf_op jit(solution)/shard_map/pallas_call | solution.py:256
  15.1 0.7 %copy.6 = bf16[128,8,128]{2,1,0:T(8,128)(2,1)} copy(bf16[128,8,128]{2,1,0:T(8,128)(2,1)S(1)} %bitcast.4) | data formatting | bytes 524288
where the time goes:
time: 15.9 us; the launch traced here: 15.8 us
  Pallas kernels  15.1 us (95%)
  local copies, waits for them, and re-layouts  0.71 us (4%)
    pallas_call x1, Pallas kernels, on_device(): pl.pallas_call(functools.partial(gather_attend, n, heads, groups, tile),...  15.1 us
    unnamed x1, local copies, waits for them, and re-layouts  0.71 us

commit v1 on v0

v1 whole, which is shorter than its diff:
```python
import functools
import math

import jax
import jax.numpy as jnp
from jax import lax
from jax.experimental import pallas as pl
from jax.experimental.pallas import tpu as pltpu
from jax.sharding import PartitionSpec as P

MESH = pl.DeviceIdType.MESH
NEG = -1e30

PLANS = (
    (((), ()),),
    ((((1, ((1, 0),), ((1, 1),)),), ((1, ((1, 0),), ((1, 1),)),)), (((0, ((0, 0),), ((0, 1),)),), ((0, ((0, 0),), ((0, 1),)),))),
    ((((1, ((1, 0), (1, 1)), ()), (2, ((2, 0),), ((2, 1),))), ((1, ((1, 0), (1, 1)), ()), (2, ((2, 0),), ((2, 1),)))), (((0, ((0, 0), (0, 1)), ()), (2, ((2, 0),), ((2, 1),))), ((0, ((0, 0), (0, 1)), ()), (2, ((2, 0),), ((2, 1),)))), (((1, ((1, 0), (1, 1)), ()), (0, ((0, 0),), ((0, 1),))), ((1, ((1, 0), (1, 1)), ()), (0, ((0, 0),), ((0, 1),))))),
    ((((1, ((1, 0), (1, 1)), ()), (2, ((2, 0), (2, 1)), ()), (3, ((3, 0),), ((3, 1),))), ((1, ((1, 0), (1, 1)), ()), (2, ((2, 0), (2, 1)), ()), (3, ((3, 0),), ((3, 1),)))), (((3, ((3, 0), (3, 1)), ()), (0, ((0, 0), (0, 1)), ()), (2, ((2, 0),), ((2, 1),))), ((3, ((3, 0), (3, 1)), ()), (0, ((0, 0), (0, 1)), ()), (2, ((2, 0),), ((2, 1),)))), (((0, ((0, 0), (0, 1)), ()), (3, ((3, 0), (3, 1)), ()), (1, ((1, 0),), ((1, 1),))), ((0, ((0, 0), (0, 1)), ()), (3, ((3, 0), (3, 1)), ()), (1, ((1, 0),), ((1, 1),)))), (((2, ((2, 0), (2, 1)), ()), (1, ((1, 0), (1, 1)), ()), (0, ((0, 0),), ((0, 1),))), ((2, ((2, 0), (2, 1)), ()), (1, ((1, 0), (1, 1)), ()), (0, ((0, 0),), ((0, 1),))))),
)


def gather_attend(
    n,
    heads,
    groups,
    tile,
    table_hbm,
    q_hbm,
    k_hbm,
    v_hbm,
    out_ref,
    table_ref,
    q_ref,
    kv_ref,
    p_ref,
    m_ref,
    l_ref,
    acc_ref,
    wide_ref,
    keys_ref,
    values_ref,
    load_sem,
    send_sem,
    recv_sem,
    ready_sem,
):
    me = lax.axis_index("seq")
    rows, width = q_ref.shape
    tokens = rows // heads
    half = tokens // 2
    per_group = heads // groups
    cols = tokens * groups
    pieces = recv_sem.shape[1]
    piece = 2 * cols // pieces
    factor_scale = width ** (-0.5) * math.log2(math.e)
    has_right, has_left = me < n - 1, me > 0
    barrier = pltpu.get_barrier_semaphore()
    odd = lax.axis_index("head") % 2 == 1
    reach = min(2, n - 1)

    loads = [
        pltpu.make_async_copy(k_hbm, kv_ref.at[me, 0], load_sem.at[0]),
        pltpu.make_async_copy(v_hbm, kv_ref.at[me, 1], load_sem.at[0]),
        pltpu.make_async_copy(table_hbm, table_ref, load_sem.at[1]),
        pltpu.make_async_copy(q_hbm, q_ref, load_sem.at[2]),
    ]
    for load in loads:
        load.start()

    def present(device):
        return (device >= 0) & (device < n)

    for k in range(1, reach + 1):

        @pl.when(present(me + k))
        def _():
            pl.semaphore_signal(barrier, inc=1, device_id={"seq": me + k}, device_id_type=MESH)

    @pl.when(has_left)
    def _():
        pl.semaphore_wait(barrier, jnp.minimum(me, reach))

    for k in range(1, reach + 1):

        @pl.when(present(me - k))
        def _():
            pl.semaphore_signal(
                ready_sem.at[k - 1], inc=1, device_id={"seq": me - k}, device_id_type=MESH
            )

    def part(shard, which):
        per = pieces // 2
        return kv_ref.at[shard, which // per, pl.ds((which % per) * piece, piece)]

    def remote(shard, which, target):
        slot = jnp.where(shard < target, shard, shard - 1)
        return pltpu.make_async_remote_copy(
            src_ref=part(shard, which),
            dst_ref=part(shard, which),
            send_sem=send_sem.at[jnp.where(target < me, 0, 1)],
            recv_sem=recv_sem.at[slot, which],
            device_id={"seq": target},
            device_id_type=MESH,
        )

    pltpu.make_async_copy(kv_ref.at[me], kv_ref.at[me], load_sem.at[0]).wait()

    for k in range(reach, 0, -1):

        @pl.when(present(me - k))
        def _():
            for which in range(pieces):
                remote(me, which, me - k).start()

    m_ref[...] = jnp.full(m_ref.shape, NEG, jnp.float32)
    l_ref[...] = jnp.zeros(l_ref.shape, jnp.float32)
    acc_ref[...] = jnp.zeros(acc_ref.shape, jnp.float32)
    loads[2].wait()
    loads[3].wait()

    lane = lax.broadcasted_iota(jnp.int32, (heads, tokens), 1)
    group = lax.broadcasted_iota(jnp.int32, (heads, tokens), 0) // per_group

    def by_group(shard, side):
        wide_ref[...] = kv_ref[shard, side].astype(jnp.float32)
        split = [wide_ref[pl.ds(g, tokens, stride=groups), :] for g in range(groups)]
        return jnp.concatenate(split, axis=0).astype(kv_ref.dtype)

    def scores(shard, keys, section, start):
        span = pl.ds((section * half + start) * heads, tile * heads)
        first, second = table_ref[2 * shard], table_ref[2 * shard + 1]
        key_pos = jnp.where(lane < half, first * half + lane, (second - 1) * half + lane)
        offset = table_ref[2 * me + section] * half + start
        raw = lax.dot_general(
            q_ref[span, :],
            keys,
            (((1,), (1,)), ((), ())),
            preferred_element_type=jnp.float32,
        )
        raw = raw.reshape(tile, heads, cols)
        shaped = raw[:, :, :tokens]
        for g in range(1, groups):
            shaped = jnp.where(group[None] == g, raw[:, :, g * tokens : (g + 1) * tokens], shaped)
        query_pos = lax.broadcasted_iota(jnp.int32, shaped.shape, 0) + offset
        shaped = jnp.where(key_pos[None] <= query_pos, shaped, NEG)
        raw = shaped.reshape(tile * heads, tokens)
        old_max = m_ref[span, :]
        new_max = jnp.maximum(old_max, jnp.max(raw, axis=-1, keepdims=True))
        fade = jnp.exp2((old_max - new_max) * factor_scale)
        weights = jnp.exp2((raw - new_max) * factor_scale)
        m_ref[span, :] = new_max
        l_ref[span, :] = l_ref[span, :] * fade + weights
        shaped = weights.reshape(tile, heads, tokens)
        spread = [jnp.where(group[None] == g, shaped, 0.0) for g in range(groups)]
        spread = jnp.concatenate(spread, axis=-1).reshape(tile * heads, cols)
        return span, spread.astype(p_ref.dtype), fade

    def whole(shard):
        keys_ref[...] = by_group(shard, 0)
        values_ref[...] = by_group(shard, 1)

        for start in range(0, tokens, tile):
            span, weights, fade = scores(shard, keys_ref[...], start // half, start % half)
            acc_ref[span, :] = acc_ref[span, :] * fade + jnp.dot(
                weights, values_ref[...], preferred_element_type=jnp.float32
            )

    whole(me)

    for k in range(1, reach + 1):

        @pl.when(present(me + k))
        def _():
            with jax.named_scope(f"ready{k}"):
                pl.semaphore_wait(ready_sem.at[k - 1], 1)
            for which in range(pieces):
                remote(me, which, me + k).start()

    def passes_right(shard):
        return has_right & (me - shard >= reach)

    def passes_left(shard):
        return has_left & (shard - me >= reach)

    def take(shard, which):
        with jax.named_scope(f"take{which}"):
            remote(shard, which, me).wait_recv()

        @pl.when(passes_right(shard))
        def _():
            remote(shard, which, me + 1).start()

        @pl.when(passes_left(shard))
        def _():
            remote(shard, which, me - 1).start()

    def settle():
        for d in range(n):
            to_left = min(d, reach) + (max(n - 1 - d - (reach - 1), 0) if d > 0 else 0)
            to_right = min(n - 1 - d, reach) + (max(d - (reach - 1), 0) if d < n - 1 else 0)

            @pl.when(me == d)
            def _():
                for side, count in enumerate((to_left, to_right)):
                    if count:
                        sent = kv_ref.at[pl.ds(0, count)]
                        pltpu.make_async_copy(sent, sent, send_sem.at[side]).wait()

    if n == 1:
        for start in range(0, tokens, tile):
            span = pl.ds(start * heads, tile * heads)
            scale = 1.0 / jnp.sum(l_ref[span, :], axis=-1, keepdims=True)
            out_ref[span, :] = (acc_ref[span, :] * scale).astype(out_ref.dtype)
        return

    early, late = range(pieces // 2), range(pieces // 2, pieces)

    if n <= len(PLANS):
        variants = [
            ((me == d) & (odd == (parity == 1)), PLANS[n - 1][d][parity])
            for d in range(n)
            for parity in range(2)
        ]

        def shard_at(index):
            return sum(jnp.where(mine, plan[index][0], 0) for mine, plan in variants)

        def takes_at(index, side):
            for mine, plan in variants:
                taken = [t for t in plan[index][1 + side]]
                if taken:

                    @pl.when(mine)
                    def _():
                        for shard, half_of in taken:
                            for which in (early, late)[half_of]:
                                take(shard, which)

        for index in range(n - 2):
            takes_at(index, 0)
            whole(shard_at(index))
        takes_at(n - 2, 0)
        last = shard_at(n - 2)
    else:
        short = jnp.minimum(me, n - 1 - me)
        middle = has_left & has_right

        def order(index):
            paired = jnp.where(index % 2 == 1, me + (index + 1) // 2, me - index // 2)
            alone = jnp.where(me < n - 1 - me, me + index - short, me - index + short)
            return jnp.where(index <= 2 * short, paired, alone)

        def take_all(index):
            for which in range(pieces):
                take(order(index), which)

        def round_of(index, carry):
            @pl.when(middle)
            def _():
                take_all(index + 1)

            whole(order(index))

            @pl.when(jnp.logical_not(middle))
            def _():
                take_all(index + 1)

            return carry

        take_all(1)
        lax.fori_loop(1, n - 2, round_of, 0)
        whole(order(n - 2))
        last = order(n - 1)
        for which in early:
            take(last, which)

        def takes_at(index, side):
            for which in late:
                take(last, which)

    keys_ref[...] = by_group(last, 0)
    for start in range(0, tokens, tile):
        span, weights, fade = scores(last, keys_ref[...], start // half, start % half)
        scale = 1.0 / jnp.sum(l_ref[span, :], axis=-1, keepdims=True)
        p_ref[span, :] = weights
        acc_ref[span, :] = acc_ref[span, :] * (fade * scale)
        l_ref[span, :] = jnp.broadcast_to(scale, (tile * heads, width))

    takes_at(n - 2, 1)
    values_ref[...] = by_group(last, 1)
    for start in range(0, tokens, tile):
        span = pl.ds(start * heads, tile * heads)
        product = jnp.dot(p_ref[span, :], values_ref[...], preferred_element_type=jnp.float32)
        out_ref[span, :] = (acc_ref[span, :] + product * l_ref[span, :]).astype(out_ref.dtype)
    settle()


def on_device(queries, keys, values, block_order):
    n = lax.axis_size("seq")
    tokens, heads, width = queries.shape
    groups = keys.shape[1]
    rows, cols = tokens * heads, tokens * groups
    tile = min(64, tokens // 2)
    pieces = 4
    anywhere = pl.BlockSpec(memory_space=pltpu.HBM)
    out = pl.pallas_call(
        functools.partial(gather_attend, n, heads, groups, tile),
        out_shape=pltpu.VMEM((rows, width), queries.dtype),
        in_specs=[anywhere] * 4,
        out_specs=pl.BlockSpec(memory_space=pltpu.VMEM),
        scratch_shapes=[
            pltpu.SMEM(block_order.shape, block_order.dtype),
            pltpu.VMEM((rows, width), queries.dtype),
            pltpu.VMEM((n, 2, cols, width), keys.dtype),
            pltpu.VMEM((rows, cols), values.dtype),
            pltpu.VMEM((rows, width), jnp.float32),
            pltpu.VMEM((rows, width), jnp.float32),
            pltpu.VMEM((rows, width), jnp.float32),
            pltpu.VMEM((cols, width), jnp.float32),
            pltpu.VMEM((cols, width), keys.dtype),
            pltpu.VMEM((cols, width), values.dtype),
            pltpu.SemaphoreType.DMA((3,)),
            pltpu.SemaphoreType.DMA((2,)),
            pltpu.SemaphoreType.DMA((max(n - 1, 1), pieces)),
            pltpu.SemaphoreType.REGULAR((2,)),
        ],
        compiler_params=pltpu.CompilerParams(collective_id=0, has_side_effects=True),
    )(
        block_order,
        queries.reshape(rows, width),
        keys.reshape(cols, width),
        values.reshape(cols, width),
    )
    return out.reshape(tokens, heads, width)


def solution(mesh):
    placed = P(("grp", "seq"), "head", None)
    return jax.shard_map(
        on_device,
        mesh=mesh,
        in_specs=(placed, placed, placed, P("grp")),
        out_specs=placed,
        check_vma=False,
    )
```

time: 15.9 us -> 14.9 us (0.937)
  Pallas kernels: 15.1 us -> 14 us
    pallas_call x1, Pallas kernels: 15.1 us -> 14 us  [on_device(): pl.pallas_call(functools.partial(gather_attend, n, heads, groups, tile),...]
where the time goes in v1:
time: 14.9 us; the launch traced here: 14.7 us
  Pallas kernels  14 us (94%)
  local copies, waits for them, and re-layouts  0.71 us (5%)
    pallas_call x1, Pallas kernels, on_device(): pl.pallas_call(functools.partial(gather_attend, n, heads, groups, tile),...  14 us
    unnamed x1, local copies, waits for them, and re-layouts  0.71 us

profile of v1, /device:TPU:0, one launch (start us, length us, event | category | flops | bytes accessed | tf_op | source)
XLA Modules:
  0.0 14.7 jit_solution(8608246466855150795)
XLA Ops:
  0.0 14.0 %shard_map.46 = bf16[1024,128]{1,0:T(8,128)(2,1)S(1)} custom-call(s32[8]{0:T(128)} %table_hbm.1, bf16[1024,128]{1,0:T(8,128)(2,1)} %bitcast.5, bf16[256,128]{1,0:T(8,128)(2,1)} %bitcast.6, bf16[256,128]{1,0:T(8,128)(2,1)} %bitcast.7), custom_call_target="tpu_custom_call" | custom-call | tf_op jit(solution)/shard_map/pallas_call | solution.py:306
  14.0 0.7 %copy.6 = bf16[128,8,128]{2,1,0:T(8,128)(2,1)} copy(bf16[128,8,128]{2,1,0:T(8,128)(2,1)S(1)} %bitcast.4) | data formatting | bytes 524288

commit v2 on v1

v2 whole, which is shorter than its diff:
```python
import functools
import math

import jax
import jax.numpy as jnp
from jax import lax
from jax.experimental import pallas as pl
from jax.experimental.pallas import tpu as pltpu
from jax.sharding import PartitionSpec as P

MESH = pl.DeviceIdType.MESH
NEG = -1e30
KEYS, VALUES = 0, 1

LINE_OF_FOUR = (
    (
        (1, 3, 2, 0, (((1, KEYS), (1, VALUES)), ((3, KEYS),), ((3, VALUES),), ((2, KEYS),), ((2, VALUES),))),
        (1, 3, 2, 1, (((1, KEYS), (1, VALUES)), ((2, KEYS),), ((3, KEYS),), ((3, VALUES),), ((2, VALUES),))),
    ),
    (
        (0, 3, 2, 1, (((0, KEYS), (0, VALUES)), ((2, KEYS),), ((3, KEYS),), ((3, VALUES),), ((2, VALUES),))),
        (3, 2, 0, 0, (((2, KEYS), (3, KEYS), (3, VALUES), (2, VALUES)), (), (), ((0, KEYS),), ((0, VALUES),))),
    ),
    (
        (0, 3, 1, 0, (((0, KEYS), (0, VALUES)), ((3, KEYS),), ((3, VALUES),), ((1, KEYS),), ((1, VALUES),))),
        (0, 3, 1, 0, (((0, KEYS), (0, VALUES)), ((3, KEYS),), ((3, VALUES),), ((1, KEYS),), ((1, VALUES),))),
    ),
    (
        (2, 1, 0, 0, (((2, KEYS), (2, VALUES)), ((1, KEYS),), ((1, VALUES),), ((0, KEYS),), ((0, VALUES),))),
        (2, 1, 0, 0, (((2, KEYS), (2, VALUES)), ((1, KEYS),), ((1, VALUES),), ((0, KEYS),), ((0, VALUES),))),
    ),
)


def gather_attend(
    n,
    heads,
    groups,
    tile,
    table_hbm,
    q_hbm,
    k_hbm,
    v_hbm,
    out_ref,
    table_ref,
    q_ref,
    kv_ref,
    p_ref,
    m_ref,
    l_ref,
    acc_ref,
    scale_ref,
    wide_ref,
    keys_ref,
    values_ref,
    load_sem,
    send_sem,
    recv_sem,
    ready_sem,
):
    me = lax.axis_index("seq")
    odd = lax.axis_index("head") % 2 == 1
    rows, width = q_ref.shape
    tokens = rows // heads
    half = tokens // 2
    per_group = heads // groups
    cols = tokens * groups
    per_side = recv_sem.shape[1] // 2
    piece = cols // per_side
    factor_scale = width ** (-0.5) * math.log2(math.e)
    has_right, has_left = me < n - 1, me > 0
    reach_left, reach_right = min(3, n - 1), min(2, n - 1)
    barrier = pltpu.get_barrier_semaphore()

    loads = [
        pltpu.make_async_copy(k_hbm, kv_ref.at[me, KEYS], load_sem.at[0]),
        pltpu.make_async_copy(v_hbm, kv_ref.at[me, VALUES], load_sem.at[0]),
        pltpu.make_async_copy(table_hbm, table_ref, load_sem.at[1]),
        pltpu.make_async_copy(q_hbm, q_ref, load_sem.at[2]),
    ]
    for load in loads:
        load.start()

    def straight_left(high, low, is_odd):
        far = high - low
        even_way = far <= reach_left
        odd_way = (far == 1) | ((far == 2) & (high == n - 1))
        return (low >= 0) & (high < n) & ((is_odd & odd_way) | (jnp.logical_not(is_odd) & even_way))

    def straight_right(low, high):
        return (low >= 0) & (high < n) & (high - low <= reach_right)

    def meets(high, low):
        return straight_left(high, low, odd) | straight_right(low, high)

    for k in range(1, reach_left + 1):

        @pl.when(meets(me + k, me))
        def _():
            pl.semaphore_signal(barrier, inc=1, device_id={"seq": me + k}, device_id_type=MESH)

    greeted = [meets(me, me - k).astype(jnp.int32) for k in range(1, reach_left + 1)]

    @pl.when(has_left)
    def _():
        pl.semaphore_wait(barrier, sum(greeted))

    for k in range(1, reach_right + 1):

        @pl.when(straight_right(me - k, me))
        def _():
            pl.semaphore_signal(
                ready_sem.at[k - 1], inc=1, device_id={"seq": me - k}, device_id_type=MESH
            )

    def remote(shard, side, index, target, source=None):
        part = kv_ref.at[shard, side, pl.ds(index * piece, piece)]
        slot = jnp.where(shard < target, shard, shard - 1)
        return pltpu.make_async_remote_copy(
            src_ref=part if source is None else source.at[pl.ds(index * piece, piece)],
            dst_ref=part,
            send_sem=send_sem.at[jnp.where(target < me, 0, 1)],
            recv_sem=recv_sem.at[slot, side * per_side + index],
            device_id={"seq": target},
            device_id_type=MESH,
        )

    def send_mine(target, allowed, sources=(None, None)):
        @pl.when(allowed)
        def _():
            for side in (KEYS, VALUES):
                for index in range(per_side):
                    remote(me, side, index, target, sources[side]).start()

    for k, rank in ((3, None), (2, False), (1, None), (2, True)):
        if k <= reach_left:
            turn = straight_left(me, me - k, odd)
            if rank is not None:
                turn &= (jnp.logical_not(odd) & (me == n - 1)) == rank
            send_mine(me - k, turn, (k_hbm, v_hbm))

    m_ref[...] = jnp.full(m_ref.shape, NEG, jnp.float32)
    l_ref[...] = jnp.zeros(l_ref.shape, jnp.float32)
    acc_ref[...] = jnp.zeros(acc_ref.shape, jnp.float32)
    pltpu.make_async_copy(kv_ref.at[me], kv_ref.at[me], load_sem.at[0]).wait()
    loads[2].wait()
    loads[3].wait()

    lane = lax.broadcasted_iota(jnp.int32, (heads, tokens), 1)
    group = lax.broadcasted_iota(jnp.int32, (heads, tokens), 0) // per_group
    spans = [(pl.ds(start * heads, tile * heads), start) for start in range(0, tokens, tile)]

    def by_group(shard, side):
        wide_ref[...] = kv_ref[shard, side].astype(jnp.float32)
        split = [wide_ref[pl.ds(g, tokens, stride=groups), :] for g in range(groups)]
        return jnp.concatenate(split, axis=0).astype(kv_ref.dtype)

    def scores(shard, span, start):
        section = start // half
        first, second = table_ref[2 * shard], table_ref[2 * shard + 1]
        key_pos = jnp.where(lane < half, first * half + lane, (second - 1) * half + lane)
        offset = table_ref[2 * me + section] * half + start % half
        raw = lax.dot_general(
            q_ref[span, :],
            keys_ref[...],
            (((1,), (1,)), ((), ())),
            preferred_element_type=jnp.float32,
        )
        raw = raw.reshape(tile, heads, cols)
        shaped = raw[:, :, :tokens]
        for g in range(1, groups):
            shaped = jnp.where(group[None] == g, raw[:, :, g * tokens : (g + 1) * tokens], shaped)
        query_pos = lax.broadcasted_iota(jnp.int32, shaped.shape, 0) + offset
        shaped = jnp.where(key_pos[None] <= query_pos, shaped, NEG)
        raw = shaped.reshape(tile * heads, tokens)
        old_max = m_ref[span, :]
        new_max = jnp.maximum(old_max, jnp.max(raw, axis=-1, keepdims=True))
        fade = jnp.exp2((old_max - new_max) * factor_scale)
        weights = jnp.exp2((raw - new_max) * factor_scale)
        m_ref[span, :] = new_max
        l_ref[span, :] = l_ref[span, :] * fade + weights
        shaped = weights.reshape(tile, heads, tokens)
        spread = [jnp.where(group[None] == g, shaped, 0.0) for g in range(groups)]
        spread = jnp.concatenate(spread, axis=-1).reshape(tile * heads, cols)
        return spread.astype(p_ref.dtype), fade

    def scale_of(span):
        high = l_ref[span, :].astype(p_ref.dtype)
        low = (l_ref[span, :] - high.astype(jnp.float32)).astype(p_ref.dtype)
        ones = jnp.ones((2 * tokens, width), p_ref.dtype)
        return 1.0 / jnp.dot(
            jnp.concatenate([high, low], axis=1), ones, preferred_element_type=jnp.float32
        )

    def whole(shard):
        keys_ref[...] = by_group(shard, KEYS)
        values_ref[...] = by_group(shard, VALUES)
        for span, start in spans:
            weights, fade = scores(shard, span, start)
            acc_ref[span, :] = acc_ref[span, :] * fade + jnp.dot(
                weights, values_ref[...], preferred_element_type=jnp.float32
            )

    def weigh(shard, place, closes):
        keys_ref[...] = by_group(shard, KEYS)
        for span, start in spans:
            weights, fade = scores(shard, span, start)
            p_ref[place, span, :] = weights
            if closes:
                scale = scale_of(span)
                scale_ref[1, span, :] = scale
                fade *= scale
                scale_ref[0, span, :] = fade
            acc_ref[span, :] = acc_ref[span, :] * fade

    def product(span, place):
        return jnp.dot(p_ref[place, span, :], values_ref[...], preferred_element_type=jnp.float32)

    def add(shard, place, scales):
        values_ref[...] = by_group(shard, VALUES)
        for span, _ in spans:
            term = product(span, place)
            if scales:
                term *= scale_ref[1, span, :]
            acc_ref[span, :] += term

    whole(me)

    far_first = (me == n - 3) & jnp.logical_not(odd)
    for k, rank in ((1, False), (2, None), (1, True)):
        if k <= reach_right:
            turn = straight_right(me, me + k)
            if rank is not None:
                turn &= far_first == rank

            @pl.when(turn)
            def _():
                pl.semaphore_wait(ready_sem.at[k - 1], 1)

            send_mine(me + k, turn)

    def take(shard, side):
        for index in range(per_side):
            remote(shard, side, index, me).wait_recv()

            @pl.when(has_right & (shard < me) & jnp.logical_not(straight_right(shard, me + 1)))
            def _():
                remote(shard, side, index, me + 1).start()

            @pl.when(has_left & (shard > me) & jnp.logical_not(straight_left(shard, me - 1, odd)))
            def _():
                remote(shard, side, index, me - 1).start()

    def settle():
        for d in range(n):
            for is_odd in (False, True):
                lefts = [s for s in range(d + 1, n) if d > 0]
                if is_odd:
                    lefts = [s for s in lefts if not (s == n - 1 and s - d == 1)]
                    own_left = min(d, 2 if d == n - 1 else 1)
                else:
                    lefts = [s for s in lefts if s - d + 1 > reach_left]
                    own_left = min(d, reach_left)
                rights = [s for s in range(d) if d < n - 1 and d + 1 - s > reach_right]
                own_right = min(n - 1 - d, reach_right)
                counts = (own_left + len(lefts), own_right + len(rights))

                @pl.when((me == d) & (odd == is_odd))
                def _():
                    for way, count in enumerate(counts):
                        if count:
                            sent = kv_ref.at[pl.ds(0, count)]
                            pltpu.make_async_copy(sent, sent, send_sem.at[way]).wait()

    if n == 1:
        for span, _ in spans:
            out_ref[span, :] = (acc_ref[span, :] * scale_of(span)).astype(out_ref.dtype)
        return

    def attend_in_turn(second, last, wait_for):
        if second is not None:
            wait_for(1)
            weigh(second, 1, False)
            wait_for(2)
            add(second, 1, False)
        wait_for(3)
        weigh(last, 0, True)

    if n == len(LINE_OF_FOUR):
        variants = [
            ((me == d) & (odd == (parity == 1)), LINE_OF_FOUR[d][parity])
            for d in range(n)
            for parity in range(2)
        ]
        first, second, last, split = (
            sum(jnp.where(mine, plan[field], 0) for mine, plan in variants) for field in range(4)
        )

        def wait_for(stage, kinds=(0, 1)):
            for mine, plan in variants:
                if plan[3] in kinds and plan[4][stage]:

                    @pl.when(mine)
                    def _():
                        for shard, side in plan[4][stage]:
                            take(shard, side)

        wait_for(0)
        whole(first)

        @pl.when(split == 0)
        def _():
            attend_in_turn(second, last, functools.partial(wait_for, kinds=(0,)))

        @pl.when(split == 1)
        def _():
            wait_for(1, (1,))
            weigh(last, 0, False)
            wait_for(2, (1,))
            weigh(second, 1, True)
            wait_for(3, (1,))
            add(second, 1, True)

        wait_for(4)
        factor = jnp.where(split == 1, 0, 1)
    else:
        short = jnp.minimum(me, n - 1 - me)

        def order(index):
            paired = jnp.where(index % 2 == 1, me + (index + 1) // 2, me - index // 2)
            alone = jnp.where(me < n - 1 - me, me + index - short, me - index + short)
            return jnp.where(index <= 2 * short, paired, alone)

        def take_both(index):
            take(order(index), KEYS)
            take(order(index), VALUES)

        def round_of(index, carry):
            take_both(index + 1)
            whole(order(index))
            return carry

        if n > 3:
            take_both(1)
            lax.fori_loop(1, n - 3, round_of, 0)
            whole(order(n - 3))
        last = order(n - 1)

        def wait_for(stage):
            take(order(n - 2) if stage < 3 else last, (stage + 1) % 2)

        attend_in_turn(order(n - 2) if n > 2 else None, last, wait_for)
        wait_for(4)
        factor = 1

    values_ref[...] = by_group(last, VALUES)
    for span, _ in spans:
        out_ref[span, :] = (acc_ref[span, :] + product(span, 0) * scale_ref[factor, span, :]).astype(
            out_ref.dtype
        )
    settle()


def on_device(queries, keys, values, block_order):
    n = lax.axis_size("seq")
    tokens, heads, width = queries.shape
    groups = keys.shape[1]
    rows, cols = tokens * heads, tokens * groups
    tile = min(64, tokens // 2)
    pieces = 4
    anywhere = pl.BlockSpec(memory_space=pltpu.HBM)
    out = pl.pallas_call(
        functools.partial(gather_attend, n, heads, groups, tile),
        out_shape=pltpu.VMEM((rows, width), queries.dtype),
        in_specs=[anywhere] * 4,
        out_specs=pl.BlockSpec(memory_space=pltpu.VMEM),
        scratch_shapes=[
            pltpu.SMEM(block_order.shape, block_order.dtype),
            pltpu.VMEM((rows, width), queries.dtype),
            pltpu.VMEM((n, 2, cols, width), keys.dtype),
            pltpu.VMEM((2, rows, cols), values.dtype),
            pltpu.VMEM((rows, width), jnp.float32),
            pltpu.VMEM((rows, width), jnp.float32),
            pltpu.VMEM((rows, width), jnp.float32),
            pltpu.VMEM((2, rows, width), jnp.float32),
            pltpu.VMEM((cols, width), jnp.float32),
            pltpu.VMEM((cols, width), keys.dtype),
            pltpu.VMEM((cols, width), values.dtype),
            pltpu.SemaphoreType.DMA((3,)),
            pltpu.SemaphoreType.DMA((2,)),
            pltpu.SemaphoreType.DMA((max(n - 1, 1), pieces)),
            pltpu.SemaphoreType.REGULAR((2,)),
        ],
        compiler_params=pltpu.CompilerParams(collective_id=0, has_side_effects=True),
    )(
        block_order,
        queries.reshape(rows, width),
        keys.reshape(cols, width),
        values.reshape(cols, width),
    )
    return out.reshape(tokens, heads, width)


def solution(mesh):
    placed = P(("grp", "seq"), "head", None)
    return jax.shard_map(
        on_device,
        mesh=mesh,
        in_specs=(placed, placed, placed, P("grp")),
        out_specs=placed,
        check_vma=False,
    )
```

time: 14.9 us -> 13.2 us (0.89)
  the two profiles are of different devices: /device:TPU:0 before, /device:TPU:1 now
where the time goes in v2:
time: 13.2 us; the launch traced here: 13 us
  Pallas kernels  12.3 us (93%)
  local copies, waits for them, and re-layouts  0.71 us (5%)
    pallas_call x1, Pallas kernels, on_device(): pl.pallas_call(functools.partial(gather_attend, n, heads, groups, tile),...  12.3 us
    unnamed x1, local copies, waits for them, and re-layouts  0.71 us

profile of v2, /device:TPU:1, one launch (start us, length us, event | category | flops | bytes accessed | tf_op | source)
XLA Modules:
  0.0 13.0 jit_solution(9359365615952867578)
XLA Ops:
  0.0 12.3 %shard_map.46 = bf16[1024,128]{1,0:T(8,128)(2,1)S(1)} custom-call(s32[8]{0:T(128)} %table_hbm.1, bf16[1024,128]{1,0:T(8,128)(2,1)} %bitcast.5, bf16[256,128]{1,0:T(8,128)(2,1)} %bitcast.6, bf16[256,128]{1,0:T(8,128)(2,1)} %bitcast.7), custom_call_target="tpu_custom_call" | custom-call | tf_op jit(solution)/shard_map/pallas_call | solution.py:372
  12.3 0.7 %copy.6 = bf16[128,8,128]{2,1,0:T(8,128)(2,1)} copy(bf16[128,8,128]{2,1,0:T(8,128)(2,1)S(1)} %bitcast.4) | data formatting | bytes 524288

commit v3 on v2

--- a/solution.py
+++ b/solution.py
@@ -155,7 +155,7 @@
         split = [wide_ref[pl.ds(g, tokens, stride=groups), :] for g in range(groups)]
         return jnp.concatenate(split, axis=0).astype(kv_ref.dtype)
 
-    def scores(shard, span, start):
+    def scores(shard, span, start, mine=False, closes=False):
         section = start // half
         first, second = table_ref[2 * shard], table_ref[2 * shard + 1]
         key_pos = jnp.where(lane < half, first * half + lane, (second - 1) * half + lane)
@@ -170,33 +170,38 @@
         shaped = raw[:, :, :tokens]
         for g in range(1, groups):
             shaped = jnp.where(group[None] == g, raw[:, :, g * tokens : (g + 1) * tokens], shaped)
-        query_pos = lax.broadcasted_iota(jnp.int32, shaped.shape, 0) + offset
-        shaped = jnp.where(key_pos[None] <= query_pos, shaped, NEG)
+        if mine:
+            query_pos = lax.broadcasted_iota(jnp.int32, shaped.shape, 0) + offset
+            shaped = jnp.where(key_pos[None] <= query_pos, shaped, NEG)
+        else:
+            shaped += jnp.where(key_pos <= offset, 0.0, NEG)[None]
         raw = shaped.reshape(tile * heads, tokens)
         old_max = m_ref[span, :]
         new_max = jnp.maximum(old_max, jnp.max(raw, axis=-1, keepdims=True))
         fade = jnp.exp2((old_max - new_max) * factor_scale)
         weights = jnp.exp2((raw - new_max) * factor_scale)
-        m_ref[span, :] = new_max
-        l_ref[span, :] = l_ref[span, :] * fade + weights
+        sums = l_ref[span, :] * fade + weights
+        if not closes:
+            m_ref[span, :] = new_max
+            l_ref[span, :] = sums
         shaped = weights.reshape(tile, heads, tokens)
         spread = [jnp.where(group[None] == g, shaped, 0.0) for g in range(groups)]
         spread = jnp.concatenate(spread, axis=-1).reshape(tile * heads, cols)
-        return spread.astype(p_ref.dtype), fade
-
-    def scale_of(span):
-        high = l_ref[span, :].astype(p_ref.dtype)
-        low = (l_ref[span, :] - high.astype(jnp.float32)).astype(p_ref.dtype)
+        return spread.astype(p_ref.dtype), fade, sums
+
+    def scale_of(sums):
+        high = sums.astype(p_ref.dtype)
+        low = (sums - high.astype(jnp.float32)).astype(p_ref.dtype)
         ones = jnp.ones((2 * tokens, width), p_ref.dtype)
         return 1.0 / jnp.dot(
             jnp.concatenate([high, low], axis=1), ones, preferred_element_type=jnp.float32
         )
 
-    def whole(shard):
+    def whole(shard, mine=False):
         keys_ref[...] = by_group(shard, KEYS)
         values_ref[...] = by_group(shard, VALUES)
         for span, start in spans:
-            weights, fade = scores(shard, span, start)
+            weights, fade, _ = scores(shard, span, start, mine)
             acc_ref[span, :] = acc_ref[span, :] * fade + jnp.dot(
                 weights, values_ref[...], preferred_element_type=jnp.float32
             )
@@ -204,13 +209,14 @@
     def weigh(shard, place, closes):
         keys_ref[...] = by_group(shard, KEYS)
         for span, start in spans:
-            weights, fade = scores(shard, span, start)
+            weights, fade, sums = scores(shard, span, start, closes=closes)
             p_ref[place, span, :] = weights
             if closes:
-                scale = scale_of(span)
-                scale_ref[1, span, :] = scale
+                scale = scale_of(sums)
                 fade *= scale
-                scale_ref[0, span, :] = fade
+                scale_ref[place, span, :] = scale
+                if place == 1:
+                    scale_ref[0, span, :] = fade
             acc_ref[span, :] = acc_ref[span, :] * fade
 
     def product(span, place):
@@ -224,7 +230,7 @@
                 term *= scale_ref[1, span, :]
             acc_ref[span, :] += term
 
-    whole(me)
+    whole(me, mine=True)
 
     far_first = (me == n - 3) & jnp.logical_not(odd)
     for k, rank in ((1, False), (2, None), (1, True)):
@@ -274,7 +280,7 @@
 
     if n == 1:
         for span, _ in spans:
-            out_ref[span, :] = (acc_ref[span, :] * scale_of(span)).astype(out_ref.dtype)
+            out_ref[span, :] = (acc_ref[span, :] * scale_of(l_ref[span, :])).astype(out_ref.dtype)
         return
 
     def attend_in_turn(second, last, wait_for):
@@ -322,7 +328,6 @@
             add(second, 1, True)
 
         wait_for(4)
-        factor = jnp.where(split == 1, 0, 1)
     else:
         short = jnp.minimum(me, n - 1 - me)
 
@@ -351,11 +356,10 @@
 
         attend_in_turn(order(n - 2) if n > 2 else None, last, wait_for)
         wait_for(4)
-        factor = 1
 
     values_ref[...] = by_group(last, VALUES)
     for span, _ in spans:
-        out_ref[span, :] = (acc_ref[span, :] + product(span, 0) * scale_ref[factor, span, :]).astype(
+        out_ref[span, :] = (acc_ref[span, :] + product(span, 0) * scale_ref[0, span, :]).astype(
             out_ref.dtype
         )
     settle()

time: 13.2 us -> 13.2 us (level)
  no operation moved by 1% of the time
where the time goes in v3:
time: 13.2 us; the launch traced here: 13 us
  Pallas kernels  12.3 us (93%)
  local copies, waits for them, and re-layouts  0.71 us (5%)
    pallas_call x1, Pallas kernels, on_device(): pl.pallas_call(functools.partial(gather_attend, n, heads, groups, tile),...  12.3 us
    unnamed x1, local copies, waits for them, and re-layouts  0.71 us

profile of v3, /device:TPU:1, one launch (start us, length us, event | category | flops | bytes accessed | tf_op | source)
XLA Modules:
  0.0 13.0 jit_solution(4718199620086065561)
XLA Ops:
  0.0 12.3 %shard_map.46 = bf16[1024,128]{1,0:T(8,128)(2,1)S(1)} custom-call(s32[8]{0:T(128)} %table_hbm.1, bf16[1024,128]{1,0:T(8,128)(2,1)} %bitcast.5, bf16[256,128]{1,0:T(8,128)(2,1)} %bitcast.6, bf16[256,128]{1,0:T(8,128)(2,1)} %bitcast.7), custom_call_target="tpu_custom_call" | custom-call | tf_op jit(solution)/shard_map/pallas_call | solution.py:376
  12.3 0.7 %copy.6 = bf16[128,8,128]{2,1,0:T(8,128)(2,1)} copy(bf16[128,8,128]{2,1,0:T(8,128)(2,1)S(1)} %bitcast.4) | data formatting | bytes 524288

commit v4 on v3

--- a/solution.py
+++ b/solution.py
@@ -76,7 +76,7 @@
         pltpu.make_async_copy(k_hbm, kv_ref.at[me, KEYS], load_sem.at[0]),
         pltpu.make_async_copy(v_hbm, kv_ref.at[me, VALUES], load_sem.at[0]),
         pltpu.make_async_copy(table_hbm, table_ref, load_sem.at[1]),
-        pltpu.make_async_copy(q_hbm, q_ref, load_sem.at[2]),
+        pltpu.make_async_copy(q_hbm, q_ref, load_sem.at[0]),
     ]
     for load in loads:
         load.start()
@@ -119,7 +119,7 @@
         return pltpu.make_async_remote_copy(
             src_ref=part if source is None else source.at[pl.ds(index * piece, piece)],
             dst_ref=part,
-            send_sem=send_sem.at[jnp.where(target < me, 0, 1)],
+            send_sem=send_sem.at[0 if send_sem.shape[0] == 1 else jnp.where(target < me, 0, 1)],
             recv_sem=recv_sem.at[slot, side * per_side + index],
             device_id={"seq": target},
             device_id_type=MESH,
@@ -142,9 +142,9 @@
     m_ref[...] = jnp.full(m_ref.shape, NEG, jnp.float32)
     l_ref[...] = jnp.zeros(l_ref.shape, jnp.float32)
     acc_ref[...] = jnp.zeros(acc_ref.shape, jnp.float32)
-    pltpu.make_async_copy(kv_ref.at[me], kv_ref.at[me], load_sem.at[0]).wait()
+    loaded = p_ref.at[0, pl.ds(0, (2 * cols + rows) * width // cols)]
+    pltpu.make_async_copy(loaded, loaded, load_sem.at[0]).wait()
     loads[2].wait()
-    loads[3].wait()
 
     lane = lax.broadcasted_iota(jnp.int32, (heads, tokens), 1)
     group = lax.broadcasted_iota(jnp.int32, (heads, tokens), 0) // per_group
@@ -273,9 +273,12 @@
 
                 @pl.when((me == d) & (odd == is_odd))
                 def _():
-                    for way, count in enumerate(counts):
-                        if count:
-                            sent = kv_ref.at[pl.ds(0, count)]
+                    if send_sem.shape[0] == 1:
+                        counts_of = (scale_ref.at[:, pl.ds(0, sum(counts) * cols // 2)],)
+                    else:
+                        counts_of = [kv_ref.at[pl.ds(0, c)] if c else None for c in counts]
+                    for way, sent in enumerate(counts_of):
+                        if sent is not None:
                             pltpu.make_async_copy(sent, sent, send_sem.at[way]).wait()
 
     if n == 1:
@@ -390,8 +393,8 @@
             pltpu.VMEM((cols, width), jnp.float32),
             pltpu.VMEM((cols, width), keys.dtype),
             pltpu.VMEM((cols, width), values.dtype),
-            pltpu.SemaphoreType.DMA((3,)),
             pltpu.SemaphoreType.DMA((2,)),
+            pltpu.SemaphoreType.DMA((1 if n <= len(LINE_OF_FOUR) else 2,)),
             pltpu.SemaphoreType.DMA((max(n - 1, 1), pieces)),
             pltpu.SemaphoreType.REGULAR((2,)),
         ],

time: 13.2 us -> 13.2 us (level)
  no operation moved by 1% of the time
where the time goes in v4:
time: 13.2 us; the launch traced here: 13 us
  Pallas kernels  12.3 us (93%)
  local copies, waits for them, and re-layouts  0.71 us (5%)
    pallas_call x1, Pallas kernels, on_device(): pl.pallas_call(functools.partial(gather_attend, n, heads, groups, tile),...  12.3 us
    unnamed x1, local copies, waits for them, and re-layouts  0.71 us

profile of v4, /device:TPU:1, one launch (start us, length us, event | category | flops | bytes accessed | tf_op | source)
XLA Modules:
  0.0 13.0 jit_solution(8617782214925868740)
XLA Ops:
  0.0 12.3 %shard_map.46 = bf16[1024,128]{1,0:T(8,128)(2,1)S(1)} custom-call(s32[8]{0:T(128)} %table_hbm.1, bf16[1024,128]{1,0:T(8,128)(2,1)} %bitcast.5, bf16[256,128]{1,0:T(8,128)(2,1)} %bitcast.6, bf16[256,128]{1,0:T(8,128)(2,1)} %bitcast.7), custom_call_target="tpu_custom_call" | custom-call | tf_op jit(solution)/shard_map/pallas_call | solution.py:379
  12.3 0.7 %copy.6 = bf16[128,8,128]{2,1,0:T(8,128)(2,1)} copy(bf16[128,8,128]{2,1,0:T(8,128)(2,1)S(1)} %bitcast.4) | data formatting | bytes 524288

commit v5 on v4

--- a/solution.py
+++ b/solution.py
@@ -72,15 +72,6 @@
     reach_left, reach_right = min(3, n - 1), min(2, n - 1)
     barrier = pltpu.get_barrier_semaphore()
 
-    loads = [
-        pltpu.make_async_copy(k_hbm, kv_ref.at[me, KEYS], load_sem.at[0]),
-        pltpu.make_async_copy(v_hbm, kv_ref.at[me, VALUES], load_sem.at[0]),
-        pltpu.make_async_copy(table_hbm, table_ref, load_sem.at[1]),
-        pltpu.make_async_copy(q_hbm, q_ref, load_sem.at[0]),
-    ]
-    for load in loads:
-        load.start()
-
     def straight_left(high, low, is_odd):
         far = high - low
         even_way = far <= reach_left
@@ -104,14 +95,6 @@
     @pl.when(has_left)
     def _():
         pl.semaphore_wait(barrier, sum(greeted))
-
-    for k in range(1, reach_right + 1):
-
-        @pl.when(straight_right(me - k, me))
-        def _():
-            pl.semaphore_signal(
-                ready_sem.at[k - 1], inc=1, device_id={"seq": me - k}, device_id_type=MESH
-            )
 
     def remote(shard, side, index, target, source=None):
         part = kv_ref.at[shard, side, pl.ds(index * piece, piece)]
@@ -138,6 +121,23 @@
             if rank is not None:
                 turn &= (jnp.logical_not(odd) & (me == n - 1)) == rank
             send_mine(me - k, turn, (k_hbm, v_hbm))
+
+    for k in range(1, reach_right + 1):
+
+        @pl.when(straight_right(me - k, me))
+        def _():
+            pl.semaphore_signal(
+                ready_sem.at[k - 1], inc=1, device_id={"seq": me - k}, device_id_type=MESH
+            )
+
+    loads = [
+        pltpu.make_async_copy(k_hbm, kv_ref.at[me, KEYS], load_sem.at[0]),
+        pltpu.make_async_copy(v_hbm, kv_ref.at[me, VALUES], load_sem.at[0]),
+        pltpu.make_async_copy(table_hbm, table_ref, load_sem.at[1]),
+        pltpu.make_async_copy(q_hbm, q_ref, load_sem.at[0]),
+    ]
+    for load in loads:
+        load.start()
 
     m_ref[...] = jnp.full(m_ref.shape, NEG, jnp.float32)
     l_ref[...] = jnp.zeros(l_ref.shape, jnp.float32)

time: 13.2 us -> 13.2 us (level)
  no operation moved by 1% of the time
where the time goes in v5:
time: 13.2 us; the launch traced here: 13 us
  Pallas kernels  12.3 us (93%)
  local copies, waits for them, and re-layouts  0.71 us (5%)
    pallas_call x1, Pallas kernels, on_device(): pl.pallas_call(functools.partial(gather_attend, n, heads, groups, tile),...  12.3 us
    unnamed x1, local copies, waits for them, and re-layouts  0.71 us

profile of v5, /device:TPU:1, one launch (start us, length us, event | category | flops | bytes accessed | tf_op | source)
XLA Modules:
  0.0 13.0 jit_solution(1946672778443731669)
XLA Ops:
  0.0 12.3 %shard_map.46 = bf16[1024,128]{1,0:T(8,128)(2,1)S(1)} custom-call(s32[8]{0:T(128)} %table_hbm.1, bf16[1024,128]{1,0:T(8,128)(2,1)} %bitcast.5, bf16[256,128]{1,0:T(8,128)(2,1)} %bitcast.6, bf16[256,128]{1,0:T(8,128)(2,1)} %bitcast.7), custom_call_target="tpu_custom_call" | custom-call | tf_op jit(solution)/shard_map/pallas_call | solution.py:379
  12.3 0.7 %copy.6 = bf16[128,8,128]{2,1,0:T(8,128)(2,1)} copy(bf16[128,8,128]{2,1,0:T(8,128)(2,1)S(1)} %bitcast.4) | data formatting | bytes 524288
